TPU v7x, 256 devices: a whole 4x4x8 slice. The times are simulated.
256 devices in a mesh: fsdp: 8 (over x, core), vocab: 32 (over y, z).
Axes of the slice: x: 4, y: 4, z: 8, core: 2. Of those that a mesh axis runs over, the one named last changes fastest.
Arguments:
- hidden_states: bfloat16 [1024, 3072], P('fsdp', 'vocab'), may hold values from -512 to 512
- head: bfloat16 [3072, 65536], P('fsdp', 'vocab'), may hold values from -0.25259074 to 0.25259074
- labels: int32 [1024], P('fsdp'), may hold values from 0 to 65535
Outputs:
- token_loss: float32 [1024], P('fsdp')
- state_grad: bfloat16 [1024, 3072], P('fsdp', 'vocab')
- head_grad: float32 [3072, 65536], P('fsdp', 'vocab')
All inputs are finite; a program needn't handle non-finite values.
Results may differ from a plain program's by a relative error of at most 0.0034.
Values may be sent and summed in bfloat16 or wider, within the bound.
A program may use at most 128 MiB of HBM per device.

v0:
```python
import jax
import jax.numpy as jnp
from jax import lax
from jax.sharding import PartitionSpec as P


def combine(stats):
    peaks, totals, targets = (stats[:, 0], stats[:, 1], stats[:, 2])
    peak = jnp.max(peaks, axis=0)
    total = jnp.sum(totals * jnp.exp(peaks - peak[None]), axis=0)
    return jnp.stack([peak, total, jnp.sum(targets, axis=0)])


def local(hidden_states, head, labels):
    fsdp, vocab = (lax.axis_size("fsdp"), lax.axis_size("vocab"))
    f, v = (lax.axis_index("fsdp"), lax.axis_index("vocab"))
    features, width = head.shape
    tokens = hidden_states.shape[0]
    share = width // fsdp
    states = lax.all_gather(hidden_states.T, "fsdp", axis=1, tiled=True)
    states = lax.all_gather(states, "vocab", axis=0, tiled=True)
    wanted = lax.all_gather(labels, "fsdp", axis=0, tiled=True)
    weights = lax.all_to_all(head, "fsdp", split_axis=1, concat_axis=0, tiled=True)
    logits = lax.dot_general(
        weights, states, (((0,), (0,)), ((), ())), preferred_element_type=jnp.float32
    )
    rows = v * width + f * share + jnp.arange(share, dtype=jnp.int32)
    hits = rows[:, None] == wanted[None, :]
    local_target = jnp.sum(jnp.where(hits, logits, jnp.float32(0.0)), axis=0)
    local_peak = jnp.max(logits, axis=0)
    local_total = jnp.sum(jnp.exp(logits - local_peak[None, :]), axis=0)
    stats = jnp.stack([local_peak, local_total, local_target])
    stats = combine(lax.all_gather(stats, "fsdp", axis=0))
    stats = combine(lax.all_gather(stats, "vocab", axis=0))
    peak, total, target = (stats[0], stats[1], stats[2])
    loss = jnp.log(total) + peak - target
    token_loss = lax.dynamic_slice_in_dim(loss, f * tokens, tokens)
    errors = (jnp.exp(logits - peak[None, :]) / total[None, :] - hits.astype(jnp.float32)).astype(
        jnp.bfloat16
    )
    errors = lax.all_gather(errors, "fsdp", axis=0, tiled=True)
    terms = jnp.dot(head, errors, preferred_element_type=jnp.float32)
    parts = vocab // fsdp
    piece = features // parts
    terms = (
        terms.reshape(parts, piece, fsdp, tokens)
        .transpose(2, 0, 1, 3)
        .reshape(vocab, piece, tokens)
    )
    summed = lax.psum_scatter(terms, "vocab", scatter_dimension=0, tiled=False).astype(jnp.bfloat16)
    moves = [
        (a * vocab + u, u // parts * vocab + parts * a + u % parts)
        for a in range(fsdp)
        for u in range(vocab)
    ]
    state_grad = lax.ppermute(summed, ("fsdp", "vocab"), moves).T
    mine = lax.dynamic_slice_in_dim(states, f * features, features)
    head_grad = lax.dot_general(
        mine, errors, (((1,), (1,)), ((), ())), preferred_element_type=jnp.float32
    )
    return (token_loss, state_grad, head_grad)


def solution(mesh):
    in_specs = (P("fsdp", "vocab"), P("fsdp", "vocab"), P("fsdp"))
    out_specs = (P("fsdp"), P("fsdp", "vocab"), P("fsdp", "vocab"))
    return jax.shard_map(local, mesh=mesh, in_specs=in_specs, out_specs=out_specs, check_vma=False)
```

profile of v0, /device:TPU:17, one launch (start us, length us, event | category | flops | bytes accessed | tf_op | source)
XLA Modules:
  0.0 458.9 jit_solution(14088944663823949947)
XLA Ops:
  7.2 0.0 all-gather.8.cloned.1.call-start
  7.2 13.9 %all_gather.24 = bf16[96,1024]{1,0:T(8,128)(2,1)} all-gather(bf16[96,128]{1,0:T(8,128)(2,1)} %bitcast.67), channel_id=1, replica_groups=mesh['fsdp'=8,'vocab'=32] {'fsdp'}, dimensions={1}, use_global_device_ids=true | all-gather | bytes 221184 | tf_op jit(solution)/shard_map/all_gather | solution.py:20
  21.1 0.0 all-gather.8.cloned.1.call-update
  21.1 2.6 copy.18
  23.7 3.8 all-to-all-start
  27.5 24.3 %all-gather.2 = s32[8,1,128]{2,1,0:T(1,128)S(1)} all-gather(s32[1,1,128]{2,1,0:T(1,128)S(1)} %bitcast.73), channel_id=1, replica_groups=mesh['fsdp'=8,'vocab'=32] {'fsdp'}, dimensions={0}, use_global_device_ids=true | all-gather | bytes 4608 | tf_op jit(solution)/shard_map/all_gather | solution.py:22
  51.9 0.0 all-to-all-done
  51.9 0.7 copy.19
  52.6 55.8 %all-gather.8.cloned.1.call-done = bf16[3072,1024]{1,0:T(8,128)(2,1)} async-done(((bf16[96,1024]{1,0:T(8,128)(2,1)}), bf16[3072,1024]{1,0:T(8,128)(2,1)}) %all-gather.8.cloned.1.call-update) | async-done | bytes 6291472 | tf_op jit(solution)/shard_map/all_gather | solution.py:21
  108.5 4.6 %fusion.15 = (f32[1024]{0:T(1024)S(1)}, f32[256,1024]{1,0:T(8,128)S(1)}) fusion(bf16[3072,256]{1,0:T(8,128)(2,1)S(1)} %bitcast.58, bf16[3072,1024]{1,0:T(8,128)(2,1)} %all-gather.8.cloned.1.call-done), kind=kOutput, calls=%fused_computation.32 | convolution fusion | flops 1610873856 | bytes 8916992 | tf_op jit(solution)/shard_map/dot_general | solution.py:24
  113.1 0.3 exponential_reduce_fusion
  113.3 14.5 %all-gather.3 = f32[8,3,1024]{2,1,0:T(4,128)S(1)} all-gather(f32[1,3,1024]{2,1,0:T(4,128)S(1)} %maximum_bitcast_fusion), channel_id=2, replica_groups=mesh['fsdp'=8,'vocab'=32] {'fsdp'}, dimensions={0}, use_global_device_ids=true | all-gather | bytes 110592 | tf_op jit(solution)/shard_map/all_gather | solution.py:33
  127.8 0.1 fusion.14
  128.0 36.4 %all-gather.4 = f32[32,3,1024]{2,1,0:T(4,128)S(1)} all-gather(f32[1,3,1024]{2,1,0:T(4,128)S(1)} %maximum_bitcast_fusion.1), channel_id=3, replica_groups=mesh['fsdp'=8,'vocab'=32] {'vocab'}, dimensions={0}, use_global_device_ids=true | all-gather | bytes 405504 | tf_op jit(solution)/shard_map/all_gather | solution.py:34
  164.4 0.3 fusion.13
  164.7 0.1 fusion.6
  164.8 1.1 fusion.2
  165.8 0.0 all-gather.10.cloned.1.call-update
  165.9 0.0 reduce-scatter.2.cloned.1.call-start
  165.9 44.8 %all-gather.10.cloned.1.call-done = bf16[2048,1024]{1,0:T(8,128)(2,1)} async-done(((bf16[256,1024]{1,0:T(8,128)(2,1)}), bf16[2048,1024]{1,0:T(8,128)(2,1)}) %all-gather.10.cloned.1.call-update) | async-done | bytes 4194320 | tf_op jit(solution)/shard_map/all_gather | solution.py:41
  210.7 4.6 %convolution_bitcast_fusion = f32[384,1024]{0,1:T(8,128)S(1)} fusion(bf16[2048,1024]{1,0:T(8,128)(2,1)} %all-gather.10.cloned.1.call-done, bf16[384,2048]{1,0:T(8,128)(2,1)S(1)} %copy-done), kind=kOutput, calls=%fused_computation.1 | convolution fusion | flops 1610612736 | bytes 7340032 | tf_op jit(solution)/shard_map/dot_general | solution.py:42
  215.3 0.5 copy.22
  215.8 0.3 copy.29
  216.1 0.1 bitcast_bitcast_fusion
  216.3 1.4 copy.23
  217.7 0.0 reduce-scatter.2.cloned.1.call-update
  217.7 0.6 dynamic_slice.6
  218.3 211.7 %reduce-scatter.2.cloned.1.call-done = f32[1,96,128]{2,1,0:T(8,128)} async-done(((f32[32,96,128]{2,1,0:T(8,128)}), f32[1,96,128]{2,1,0:T(8,128)}) %reduce-scatter.2.cloned.1.call-update) | async-done | bytes 49168 | tf_op jit(solution)/shard_map/reduce_scatter | solution.py:50
  430.0 0.8 convert_bitcast_fusion
  430.8 15.1 %collective-permute-start = (bf16[96,128]{1,0:T(8,128)(2,1)S(1)}, bf16[96,128]{1,0:T(8,128)(2,1)S(1)}, u32[]{:S(2)}, u32[]{:S(2)}) collective-permute-start(bf16[96,128]{1,0:T(8,128)(2,1)S(1)} %convert_bitcast_fusion), channel_id=1, source_target_pairs={{0,0},{1,1},{2,2},{3,3},{4,32},{5,33},{6,34},{7,35},{8,64},{9,65},... | collective-permute-start | bytes 73736 | tf_op jit(solution)/shard_map/ppermute | solution.py:56
  445.8 5.9 %fusion.3 = f32[384,2048]{1,0:T(8,128)} fusion(bf16[2048,1024]{1,0:T(8,128)(2,1)} %all-gather.10.cloned.1.call-done, bf16[3072,1024]{1,0:T(8,128)(2,1)} %all-gather.8.cloned.1.call-done, s32[]{:T(128)S(6)} %select_n.12), kind=kOutput, calls=%fused_computation.8 | convolution fusion | flops 1610612736 | bytes 8126468 | tf_op jit(solution)/shard_map/dot_general | solution.py:58
  451.8 0.6 copy.47
  (11 shorter events, 0.1 us)
Async XLA Ops:
  7.2 101.3 %all-gather.8.cloned.1.call-start = ((), (), s32[]{:S(2)}) async-start(), calls=%async_computation.2 | async-start | bytes 6488064 | tf_op jit(solution)/shard_map/all_gather | solution.py:21
  23.7 3.8 copy-start.1
  23.7 28.1 %all-to-all-start = ((bf16[384,8,256]{0,2,1:T(8,128)(2,1)}), bf16[384,8,256]{0,2,1:T(8,128)(2,1)S(1)}, u32[]{:S(2)}, u32[]{:S(2)}) async-start(bf16[384,8,256]{0,2,1:T(8,128)(2,1)} %bitcast), calls=%async_computation | async-start | bytes 3145728 | tf_op jit(solution)/shard_map/all_to_all | solution.py:23
  27.5 183.2 %all-gather.10.cloned.1.call-start = ((), (), s32[]{:S(2)}) async-start(), calls=%async_computation.3 | async-start | bytes 4718592 | tf_op jit(solution)/shard_map/all_gather | solution.py:41
  164.4 46.4 %copy-start = (bf16[384,2048]{1,0:T(8,128)(2,1)S(1)}, bf16[384,2048]{1,0:T(8,128)(2,1)}, u32[]{:S(2)}) copy-start(bf16[384,2048]{1,0:T(8,128)(2,1)} %param.4) | copy-start | bytes 4718596
  165.9 264.1 %reduce-scatter.2.cloned.1.call-start = ((), (), s32[]{:S(2)}) async-start(), calls=%async_computation.4 | async-start | bytes 1622016 | tf_op jit(solution)/shard_map/reduce_scatter | solution.py:50
  430.8 21.0 %collective-permute-start = (bf16[96,128]{1,0:T(8,128)(2,1)S(1)}, bf16[96,128]{1,0:T(8,128)(2,1)S(1)}, u32[]{:S(2)}, u32[]{:S(2)}) collective-permute-start(bf16[96,128]{1,0:T(8,128)(2,1)S(1)} %convert_bitcast_fusion), channel_id=1, source_target_pairs={{0,0},{1,1},{2,2},{3,3},{4,32},{5,33},{6,34},{7,35},{8,64},{9,65},... | collective-permute-start | bytes 73736 | tf_op jit(solution)/shard_map/ppermute | solution.py:56
Sparse Core Ops, SparseCore 0:
  21.3 87.1 all-gather.7
  166.0 44.6 all-gather.9
  217.8 212.0 reduce-scatter.1
where the time goes:
time: 459 us
  waiting for transfers between devices  312 us (68%)
  blocking collectives  89.1 us (19%)
  starting transfers between devices  18.9 us (4%)
  matrix products  15.1 us (3%)
  between operations  13.8 us (3%)
  local copies, waits for them, and re-layouts  6.86 us (1%)
    reduce_scatter x1, waiting for transfers between devices, local(): lax.psum_scatter(terms, 'vocab', scatter_dimension=0, tiled=False)  212 us
    all_gather x1, waiting for transfers between devices, local(): states = lax.all_gather(states, 'vocab', axis=0, tiled=True)  55.8 us
    all_gather x1, waiting for transfers between devices, local(): errors = lax.all_gather(errors, 'fsdp', axis=0, tiled=True)  44.8 us
    all_gather x1, blocking collectives, local(): stats = combine(lax.all_gather(stats, 'vocab', axis=0))  36.4 us
    all_gather x1, blocking collectives, local(): wanted = lax.all_gather(labels, 'fsdp', axis=0, tiled=True)  24.3 us
    ppermute x1, starting transfers between devices, local(): state_grad = lax.ppermute(summed, ('fsdp', 'vocab'), moves).T  15.1 us
    all_gather x1, blocking collectives, local(): stats = combine(lax.all_gather(stats, 'fsdp', axis=0))  14.5 us
    all_gather x1, blocking collectives, local(): states = lax.all_gather(hidden_states.T, 'fsdp', axis=1, tiled=True)  13.9 us
  transfers between devices with their start and end apart: 5, of which 3 were waited for; matrix products, arithmetic and copies ran while one was open for 2% of the time, Pallas kernels for 0%

commit v1 on v0

--- a/solution.py
+++ b/solution.py
@@ -18,7 +18,9 @@
     tokens = hidden_states.shape[0]
     share = width // fsdp
     states = lax.all_gather(hidden_states.T, "fsdp", axis=1, tiled=True)
-    states = lax.all_gather(states, "vocab", axis=0, tiled=True)
+    states = jnp.concatenate(
+        lax.all_to_all(jnp.stack([states] * lax.axis_size("vocab")), "vocab", 0, 0), axis=0
+    )
     wanted = lax.all_gather(labels, "fsdp", axis=0, tiled=True)
     weights = lax.all_to_all(head, "fsdp", split_axis=1, concat_axis=0, tiled=True)
     logits = lax.dot_general(

time: 459 us -> 549 us (1.20)
  waiting for transfers between devices: 312 us -> 387 us
  starting transfers between devices: 18.9 us -> 31.6 us
    all_to_all x0 -> x1, waiting for transfers between devices: none -> 131 us  [local(): lax.all_to_all(jnp.stack([states] * lax.axis_size('vocab')), 'vocab', 0, 0)]
    all_gather x1 -> x0, waiting for transfers between devices: 55.8 us -> none  [local(): states = lax.all_gather(states, 'vocab', axis=0, tiled=True)]
    all_gather x1, blocking collectives: 24.3 us -> 10 us  [local(): wanted = lax.all_gather(labels, 'fsdp', axis=0, tiled=True)]
    all_gather x1, blocking collectives: 13.9 us -> 27 us  [local(): states = lax.all_gather(hidden_states.T, 'fsdp', axis=1, tiled=True)]
    all_to_all x0 -> x1, starting transfers between devices: none -> 11.2 us  [local(): lax.all_to_all(jnp.stack([states] * lax.axis_size('vocab')), 'vocab', 0, 0)]
  transfers between devices with their start and end apart: 5 -> 5, of which waited for: 3 -> 3; matrix products, arithmetic and copies ran while one was open for 2% -> 1% of each run, Pallas kernels for 0% -> 0%
where the time goes in v1:
time: 549 us
  waiting for transfers between devices  387 us (70%)
  blocking collectives  88.2 us (16%)
  starting transfers between devices  31.6 us (6%)
  matrix products  15.2 us (3%)
  between operations  14.2 us (3%)
  local copies, waits for them, and re-layouts  10.3 us (2%)
    reduce_scatter x1, waiting for transfers between devices, local(): lax.psum_scatter(terms, 'vocab', scatter_dimension=0, tiled=False)  212 us
    all_to_all x1, waiting for transfers between devices, local(): lax.all_to_all(jnp.stack([states] * lax.axis_size('vocab')), 'vocab', 0, 0)  131 us
    all_gather x1, waiting for transfers between devices, local(): errors = lax.all_gather(errors, 'fsdp', axis=0, tiled=True)  44.5 us
    all_gather x1, blocking collectives, local(): stats = combine(lax.all_gather(stats, 'vocab', axis=0))  37.4 us
    all_gather x1, blocking collectives, local(): states = lax.all_gather(hidden_states.T, 'fsdp', axis=1, tiled=True)  27 us
    ppermute x1, starting transfers between devices, local(): state_grad = lax.ppermute(summed, ('fsdp', 'vocab'), moves).T  15.2 us
    all_gather x1, blocking collectives, local(): stats = combine(lax.all_gather(stats, 'fsdp', axis=0))  13.9 us
    all_to_all x1, starting transfers between devices, local(): lax.all_to_all(jnp.stack([states] * lax.axis_size('vocab')), 'vocab', 0, 0)  11.2 us
  transfers between devices with their start and end apart: 5, of which 3 were waited for; matrix products, arithmetic and copies ran while one was open for 1% of the time, Pallas kernels for 0%

profile of v1, /device:TPU:17, one launch (start us, length us, event | category | flops | bytes accessed | tf_op | source)
XLA Modules:
  0.0 548.8 jit_solution(15614455325541410461)
XLA Ops:
  7.2 2.6 copy.18
  9.7 5.1 all-to-all-start
  14.9 27.0 %all_gather.21 = bf16[96,1024]{1,0:T(8,128)(2,1)S(1)} all-gather(bf16[96,128]{1,0:T(8,128)(2,1)S(1)} %bitcast.68), channel_id=1, replica_groups=mesh['fsdp'=8,'vocab'=32] {'fsdp'}, dimensions={1}, use_global_device_ids=true | all-gather | bytes 221184 | tf_op jit(solution)/shard_map/all_gather | solution.py:20
  41.8 3.5 stack.18
  45.3 11.2 %all-to-all-start.1 = ((bf16[32,96,1024]{2,1,0:T(8,128)(2,1)}), bf16[32,96,1024]{2,1,0:T(8,128)(2,1)}, u32[]{:S(2)}, u32[]{:S(2)}) async-start(bf16[32,96,1024]{2,1,0:T(8,128)(2,1)} %stack.18), calls=%async_computation.1 | async-start | bytes 12582912 | tf_op jit(solution)/shard_map/all_to_all | solution.py:22
  56.5 0.0 all-gather.7.cloned.1.call-start
  56.6 10.0 %all-gather.2 = s32[8,1,128]{2,1,0:T(1,128)S(1)} all-gather(s32[1,1,128]{2,1,0:T(1,128)S(1)} %bitcast.74), channel_id=1, replica_groups=mesh['fsdp'=8,'vocab'=32] {'fsdp'}, dimensions={0}, use_global_device_ids=true | all-gather | bytes 4608 | tf_op jit(solution)/shard_map/all_gather | solution.py:24
  66.6 0.7 copy.19
  67.3 130.6 %all-to-all-done.1 = bf16[32,96,1024]{2,1,0:T(8,128)(2,1)} async-done(((bf16[32,96,1024]{2,1,0:T(8,128)(2,1)}), bf16[32,96,1024]{2,1,0:T(8,128)(2,1)}, u32[]{:S(2)}, u32[]{:S(2)}) %all-to-all-start.1) | async-done | bytes 6291488 | tf_op jit(solution)/shard_map/all_to_all | solution.py:22
  197.9 4.6 fusion.15
  202.6 0.3 exponential_reduce_fusion
  202.9 13.9 %all-gather.3 = f32[8,3,1024]{2,1,0:T(4,128)S(1)} all-gather(f32[1,3,1024]{2,1,0:T(4,128)S(1)} %maximum_bitcast_fusion), channel_id=2, replica_groups=mesh['fsdp'=8,'vocab'=32] {'fsdp'}, dimensions={0}, use_global_device_ids=true | all-gather | bytes 110592 | tf_op jit(solution)/shard_map/all_gather | solution.py:35
  216.7 0.1 fusion.14
  216.9 37.4 %all-gather.4 = f32[32,3,1024]{2,1,0:T(4,128)S(1)} all-gather(f32[1,3,1024]{2,1,0:T(4,128)S(1)} %maximum_bitcast_fusion.1), channel_id=3, replica_groups=mesh['fsdp'=8,'vocab'=32] {'vocab'}, dimensions={0}, use_global_device_ids=true | all-gather | bytes 405504 | tf_op jit(solution)/shard_map/all_gather | solution.py:36
  254.3 0.3 fusion.13
  254.6 0.1 fusion.6
  254.7 1.1 fusion.2
  255.8 0.0 all-gather.7.cloned.1.call-update
  255.8 0.0 reduce-scatter.2.cloned.1.call-start
  255.8 44.5 %all-gather.7.cloned.1.call-done = bf16[2048,1024]{1,0:T(8,128)(2,1)} async-done(((bf16[256,1024]{1,0:T(8,128)(2,1)}), bf16[2048,1024]{1,0:T(8,128)(2,1)}) %all-gather.7.cloned.1.call-update) | async-done | bytes 4194320 | tf_op jit(solution)/shard_map/all_gather | solution.py:43
  300.3 4.6 convolution_bitcast_fusion
  304.9 0.5 copy.22
  305.4 0.3 copy.29
  305.8 0.1 bitcast_bitcast_fusion
  305.9 1.4 copy.23
  307.3 0.0 reduce-scatter.2.cloned.1.call-update
  307.3 0.6 dynamic_slice.6
  307.9 211.5 %reduce-scatter.2.cloned.1.call-done = f32[1,96,128]{2,1,0:T(8,128)} async-done(((f32[32,96,128]{2,1,0:T(8,128)}), f32[1,96,128]{2,1,0:T(8,128)}) %reduce-scatter.2.cloned.1.call-update) | async-done | bytes 49168 | tf_op jit(solution)/shard_map/reduce_scatter | solution.py:52
  519.5 0.8 convert_bitcast_fusion
  520.3 15.2 %collective-permute-start = (bf16[96,128]{1,0:T(8,128)(2,1)S(1)}, bf16[96,128]{1,0:T(8,128)(2,1)S(1)}, u32[]{:S(2)}, u32[]{:S(2)}) collective-permute-start(bf16[96,128]{1,0:T(8,128)(2,1)S(1)} %convert_bitcast_fusion), channel_id=1, source_target_pairs={{0,0},{1,1},{2,2},{3,3},{4,32},{5,33},{6,34},{7,35},{8,64},{9,65},... | collective-permute-start | bytes 73736 | tf_op jit(solution)/shard_map/ppermute | solution.py:58
  535.5 5.9 %fusion.3 = f32[384,2048]{1,0:T(8,128)} fusion(bf16[2048,1024]{1,0:T(8,128)(2,1)} %all-gather.7.cloned.1.call-done, bf16[3072,1024]{1,0:T(8,128)(2,1)} %bitcast.4, s32[]{:T(128)S(6)} %select_n.12), kind=kOutput, calls=%fused_computation.8 | convolution fusion | flops 1610612736 | bytes 8126468 | tf_op jit(solution)/shard_map/dot_general | solution.py:60
  541.4 0.6 copy.47
  (13 shorter events, 0.1 us)
Async XLA Ops:
  9.7 5.1 copy-start.1
  9.7 32.1 %all-to-all-start = ((bf16[384,8,256]{0,2,1:T(8,128)(2,1)}), bf16[384,8,256]{0,2,1:T(8,128)(2,1)S(1)}, u32[]{:S(2)}, u32[]{:S(2)}) async-start(bf16[384,8,256]{0,2,1:T(8,128)(2,1)} %bitcast), calls=%async_computation | async-start | bytes 3145728 | tf_op jit(solution)/shard_map/all_to_all | solution.py:25
  45.3 11.3 %copy-start.2 = (s32[128]{0:T(128)S(1)}, s32[128]{0:T(128)}, u32[]{:S(2)}) copy-start(s32[128]{0:T(128)} %param.5) | copy-start | bytes 1540
  45.3 152.7 %all-to-all-start.1 = ((bf16[32,96,1024]{2,1,0:T(8,128)(2,1)}), bf16[32,96,1024]{2,1,0:T(8,128)(2,1)}, u32[]{:S(2)}, u32[]{:S(2)}) async-start(bf16[32,96,1024]{2,1,0:T(8,128)(2,1)} %stack.18), calls=%async_computation.1 | async-start | bytes 12582912 | tf_op jit(solution)/shard_map/all_to_all | solution.py:22
  56.5 243.8 %all-gather.7.cloned.1.call-start = ((), (), s32[]{:S(2)}) async-start(), calls=%async_computation.3 | async-start | bytes 4718592 | tf_op jit(solution)/shard_map/all_gather | solution.py:43
  254.3 46.0 %copy-start = (bf16[384,2048]{1,0:T(8,128)(2,1)S(1)}, bf16[384,2048]{1,0:T(8,128)(2,1)}, u32[]{:S(2)}) copy-start(bf16[384,2048]{1,0:T(8,128)(2,1)} %param.4) | copy-start | bytes 4718596
  255.8 263.7 %reduce-scatter.2.cloned.1.call-start = ((), (), s32[]{:S(2)}) async-start(), calls=%async_computation.4 | async-start | bytes 1622016 | tf_op jit(solution)/shard_map/reduce_scatter | solution.py:52
  520.3 21.1 %collective-permute-start = (bf16[96,128]{1,0:T(8,128)(2,1)S(1)}, bf16[96,128]{1,0:T(8,128)(2,1)S(1)}, u32[]{:S(2)}, u32[]{:S(2)}) collective-permute-start(bf16[96,128]{1,0:T(8,128)(2,1)S(1)} %convert_bitcast_fusion), channel_id=1, source_target_pairs={{0,0},{1,1},{2,2},{3,3},{4,32},{5,33},{6,34},{7,35},{8,64},{9,65},... | collective-permute-start | bytes 73736 | tf_op jit(solution)/shard_map/ppermute | solution.py:58
Sparse Core Ops, SparseCore 0:
  255.9 44.3 all-gather.6
  307.4 211.9 reduce-scatter.1
